TPU v7x, 8 devices: a whole 2x2x1 slice. The times are simulated.
8 devices in a mesh: dp: 2 (over z, y), stage: 2 (over x), tp: 2 (over core).
Axes of the slice: x: 2, y: 2, z: 1, core: 2. Of those that a mesh axis runs over, the one named last changes fastest.
Arguments:
- act_in: bfloat16 [2, 24, 28, 28, 512], P('stage', ('dp', 'tp'))
- w_conv: bfloat16 [2, 3, 3, 512, 512], P('stage', None, None, 'tp')
- w_short: bfloat16 [2, 512, 512], P('stage', 'tp')
- gamma: float32 [2, 512], P('stage', 'tp')
- beta: float32 [2, 512], P('stage', 'tp')
- gamma_s: float32 [2, 512], P('stage', 'tp')
- grad_z: bfloat16 [2, 24, 28, 28, 512], P('stage', 'dp', None, None, 'tp')
Outputs:
- output 1: bfloat16 [2, 24, 28, 28, 512], P('stage', 'dp', None, None, 'tp')
- output 2: bfloat16 [2, 24, 28, 28, 512], P('stage', ('dp', 'tp'))
- output 3: float32 [2, 3, 3, 512, 512], P('stage', None, None, 'tp')
- output 4: float32 [2, 512, 512], P('stage', 'tp')
All inputs are finite; a program needn't handle non-finite values.
Results may differ from a plain program's by a relative error of at most 0.00383.
Values are sent between devices in bfloat16 or wider.
A program may use at most 1 GiB of HBM per device.

v0:
```python
import jax
import jax.numpy as jnp
from jax import lax
from jax.sharding import PartitionSpec as P


def conv_same(left_op, right_op, right_spec):
    return lax.conv_general_dilated(left_op, right_op, (1, 1), "SAME", dimension_numbers=("NHWC", right_spec, "NHWC"), preferred_element_type=jnp.float32)


def weight_grad(images_in, grads_out):
    return lax.conv_general_dilated(images_in, grads_out, (1, 1), ((1, 1), (1, 1)), dimension_numbers=("CHWN", "IHWO", "HWNC"), preferred_element_type=jnp.float32)


def solution(mesh):
    act_spec = P("stage", ("dp", "tp"), None, None, None)
    kernel_spec = P("stage", None, None, "tp", None)
    short_spec = P("stage", "tp", None)
    vec_spec = P("stage", "tp")
    grad_spec = P("stage", "dp", None, None, "tp")

    def device_step(act_in, w_conv, w_short, gamma, beta, gamma_s, grad_z):
        by_channel = lax.all_to_all(act_in[0], "tp", 3, 0, tiled=True)
        act_local = lax.ppermute(by_channel, "stage", perm=[(0, 1)])
        kernel = w_conv[0]
        short_w = w_short[0]
        scale_main = gamma[0]
        shift_main = beta[0]
        scale_short = gamma_s[0]
        pre_part = conv_same(act_local, kernel, "HWIO")
        short_part = jnp.einsum("nhwc,co->nhwo", act_local, short_w, preferred_element_type=jnp.float32)
        pre_sum, short_sum = lax.psum_scatter((pre_part, short_part), "tp", scatter_dimension=3, tiled=True)
        mixed_sum = pre_sum * scale_main + shift_main + short_sum * scale_short
        z_val = jnp.maximum(mixed_sum, 0.0).astype(jnp.bfloat16)
        mask_pos = mixed_sum > 0.0
        grad_here = grad_z[0]
        g_main = jnp.where(mask_pos, grad_here * scale_main, 0.0).astype(jnp.bfloat16)
        g_short = jnp.where(mask_pos, grad_here * scale_short, 0.0).astype(jnp.bfloat16)
        g_main_all, g_short_all = lax.all_gather((g_main, g_short), "tp", axis=3, tiled=True)
        grad_wide = conv_same(g_main_all, kernel[::-1, ::-1], "HWOI") + jnp.einsum("nhwo,co->nhwc", g_short_all, short_w, preferred_element_type=jnp.float32)
        grad_local = grad_wide.astype(jnp.bfloat16)
        dw_part = weight_grad(act_local, g_main_all)
        dws_part = jnp.einsum("nhwc,nhwo->co", act_local, g_short_all, preferred_element_type=jnp.float32)
        dw_sum, dws_sum = lax.psum((dw_part, dws_part), "dp")
        returned = lax.ppermute(grad_local, "stage", perm=[(1, 0)])
        grad_act = lax.all_to_all(returned, "tp", 0, 3, tiled=True)
        return z_val[None], grad_act[None], dw_sum[None], dws_sum[None]

    return jax.shard_map(device_step, mesh=mesh, in_specs=(act_spec, kernel_spec, short_spec, vec_spec, vec_spec, vec_spec, grad_spec), out_specs=(grad_spec, act_spec, kernel_spec, short_spec), check_vma=False)
```

profile of v0, /device:TPU:0, one launch (start us, length us, event | category | flops | bytes accessed | tf_op | source)
XLA Modules:
  0.0 750.4 jit_solution(12693835678733932273)
XLA Ops:
  7.2 0.0 copy-start
  7.2 0.0 reduce-scatter.5.cloned.1.call-start
  7.2 40.0 %copy.61 = bf16[1,6,28,28,512]{3,2,1,4,0:T(8,128)(2,1)} copy(bf16[1,6,28,28,512]{4,3,2,1,0:T(8,128)(2,1)} %param.7) | data formatting | bytes 9633792 | tf_op args[0]
  47.3 22.2 %bitcast_bitcast_fusion = bf16[512,6,28,28]{3,2,1,0:T(8,128)(2,1)} fusion(bf16[1,6,28,28,512]{3,2,1,4,0:T(8,128)(2,1)} %copy.61), kind=kLoop, calls=%fused_computation.29 | loop fusion | bytes 9633792
  69.5 41.2 %reshape.17 = bf16[2,2,602112]{2,1,0:T(2,128)(2,1)} reshape(bf16[512,6,28,28]{3,2,1,0:T(8,128)(2,1)} %bitcast_bitcast_fusion) | data formatting | bytes 9633792
  110.7 12.9 %all_to_all.33 = bf16[2,2,602112]{2,1,0:T(2,128)(2,1)} all-to-all(bf16[2,2,602112]{2,1,0:T(2,128)(2,1)} %reshape.17), channel_id=1, replica_groups=mesh['dp'=2,'stage'=2,'tp'=2] {'tp'}, dimensions={0} | all-to-all | bytes 9633792 | tf_op jit(solution)/shard_map/all_to_all | solution.py:23
  123.5 37.4 %reshape.18 = bf16[512,6,28,28]{3,2,1,0:T(8,128)(2,1)} reshape(bf16[2,2,602112]{2,1,0:T(2,128)(2,1)} %all_to_all.33) | data formatting | bytes 9633792
  160.9 39.0 %copy.77 = bf16[6,28,28,2,256]{4,3,2,1,0:T(2,128)(2,1)} copy(bf16[6,28,28,2,256]{2,1,0,4,3:T(8,128)(2,1)} %bitcast.47) | data formatting | bytes 9633792 | tf_op jit(solution)/shard_map/all_to_all | solution.py:23
  199.9 0.0 copy-start.1
  199.9 3.5 copy.63
  203.5 7.4 collective-permute-start
  210.9 115.7 %collective-permute-done = bf16[12,28,28,256]{3,2,1,0:T(8,128)(2,1)} collective-permute-done((bf16[12,28,28,256]{3,2,1,0:T(8,128)(2,1)S(1)}, bf16[12,28,28,256]{3,2,1,0:T(8,128)(2,1)}, u32[]{:S(2)}, u32[]{:S(2)}) %collective-permute-start) | collective-permute-done | bytes 4816928 | tf_op jit(solution)/shard_map/ppermute | solution.py:24
  326.6 0.0 copy-done.1
  326.6 5.0 fusion.29
  331.6 16.8 %copy.65 = f32[12,28,28,512]{3,0,2,1:T(8,128)} copy(f32[12,28,28,512]{3,2,1,0:T(8,128)S(1)} %fusion.29) | data formatting | bytes 38535168 | tf_op jit(solution)/shard_map/nhwc,co->nhwo/dot_general | solution.py:31
  348.4 0.0 reduce-scatter.5.cloned.1.call-update
  348.5 0.0 reduce-scatter.3.cloned.1.call-start
  348.5 0.0 copy-done
  348.5 35.0 %fusion.12 = f32[12,28,28,512]{3,0,2,1:T(8,128)} fusion(bf16[12,28,28,256]{3,2,1,0:T(8,128)(2,1)} %collective-permute-done, bf16[1,3,3,256,512]{4,3,2,1,0:T(8,128)(2,1)S(1)} %copy-done), kind=kOutput, calls=%fused_computation.18 | convolution fusion | flops 21151875072 | bytes 26443776 | tf_op jit(solution)/shard_map/conv_general_dilated | solution.py:8
  383.5 0.0 copy-start.3
  383.5 0.0 copy-start.4
  383.5 0.0 copy-start.5
  383.5 0.0 reduce-scatter.3.cloned.1.call-update
  383.5 0.0 all-gather.5.cloned.1.call-start
  383.6 0.0 reduce-scatter.5.cloned.1.call-done
  383.6 29.3 %reduce-scatter.3.cloned.1.call-done = f32[12,28,28,256]{3,0,2,1:T(8,128)} async-done(((f32[12,28,28,512]{3,0,2,1:T(8,128)}), f32[12,28,28,256]{3,0,2,1:T(8,128)}) %reduce-scatter.3.cloned.1.call-update) | async-done | bytes 9633808 | tf_op jit(solution)/shard_map/reduce_scatter | solution.py:32
  412.9 0.0 copy-done.3
  412.9 0.0 copy-done.4
  412.9 0.0 copy-done.5
  412.9 17.2 %fusion.3 = (bf16[12,28,28,256]{3,0,2,1:T(8,128)(2,1)}, pred[12,28,28,256]{3,0,2,1:T(8,128)(4,1)}, bf16[1,12,28,28,256]{4,1,3,2,0:T(8,128)(2,1)}) fusion(f32[256]{0:T(256)S(1)} %bitcast.53, bf16[1,12,28,28,256]{4,3,2,1,0:T(8,128)(2,1)} %param.13, f32[12,28,28,256]{3,0,2,1:T(8,128)} %reduce-scatter.5.cloned.1.call-done, f32[256]{0:T(256)S(1)} %bitcast.54, ...), kind=kLoop, calls=%fused_computation.5 | loop fusion | flops 26492928 | bytes 36129792 | tf_op jit(solution)/shard_map/convert_element_type | solution.py:38
  430.1 0.0 all-gather.5.cloned.1.call-update
  430.1 0.0 all-gather.3.cloned.1.call-start
  430.2 14.7 %fusion.1 = bf16[12,28,28,256]{3,0,2,1:T(8,128)(2,1)} fusion(pred[12,28,28,256]{3,0,2,1:T(8,128)(4,1)} %get-tuple-element.27, f32[256]{0:T(256)S(1)} %bitcast.52, bf16[1,12,28,28,256]{4,3,2,1,0:T(8,128)(2,1)} %param.13), kind=kLoop, calls=%fused_computation.3 | loop fusion | flops 9633792 | bytes 12043264 | tf_op jit(solution)/shard_map/convert_element_type | solution.py:37
  444.8 0.0 all-gather.3.cloned.1.call-update
  444.9 0.2 all-reduce.3.cloned.1.call-start
  445.1 9.4 %all-gather.5.cloned.1.call-done = bf16[12,28,28,512]{3,0,2,1:T(8,128)(2,1)} async-done(((bf16[12,28,28,256]{3,0,2,1:T(8,128)(2,1)}), bf16[12,28,28,512]{3,0,2,1:T(8,128)(2,1)}) %all-gather.5.cloned.1.call-update) | async-done | bytes 9633808 | tf_op jit(solution)/shard_map/all_gather | solution.py:39
  454.5 13.1 %fusion.23 = f32[1,256,512]{1,2,0:T(8,128)} fusion(bf16[12,28,28,256]{3,2,1,0:T(8,128)(2,1)} %collective-permute-done, bf16[12,28,28,512]{3,0,2,1:T(8,128)(2,1)} %all-gather.5.cloned.1.call-done), kind=kOutput, calls=%fused_computation.25 | convolution fusion | flops 2466250752 | bytes 14974976 | tf_op jit(solution)/shard_map/nhwc,nhwo->co/dot_general | solution.py:43
  467.5 12.6 %all-gather.3.cloned.1.call-done = bf16[12,28,28,512]{3,0,2,1:T(8,128)(2,1)} async-done(((bf16[12,28,28,256]{3,0,2,1:T(8,128)(2,1)}), bf16[12,28,28,512]{3,0,2,1:T(8,128)(2,1)}) %all-gather.3.cloned.1.call-update) | async-done | bytes 9633808 | tf_op jit(solution)/shard_map/all_gather | solution.py:39
  480.1 35.9 %fusion.18 = f32[1,3,3,256,512]{4,3,2,1,0:T(8,128)} fusion(bf16[12,28,28,512]{3,0,2,1:T(8,128)(2,1)} %all-gather.3.cloned.1.call-done, bf16[12,28,28,256]{3,2,1,0:T(8,128)(2,1)} %collective-permute-done), kind=kOutput, calls=%fused_computation.24 | convolution fusion | flops 21151875072 | bytes 19169280 | tf_op jit(solution)/shard_map/conv_general_dilated | solution.py:12
  516.1 0.0 all-reduce.3.cloned.1.call-update
  516.1 0.0 copy-start.2
  516.1 35.4 %fusion.15 = f32[12,28,28,256]{3,0,2,1:T(8,128)} fusion(bf16[12,28,28,512]{3,0,2,1:T(8,128)(2,1)} %all-gather.3.cloned.1.call-done, bf16[1,3,3,256,512]{4,3,2,1,0:T(8,128)(2,1)S(1)} %copy-done), kind=kOutput, calls=%fused_computation.21 | convolution fusion | flops 21151875072 | bytes 21626880 | tf_op jit(solution)/shard_map/conv_general_dilated | solution.py:8
  551.5 0.0 copy-done.2
  551.5 26.7 %fusion.6 = bf16[12,28,28,256]{3,2,1,0:T(8,128)(2,1)} fusion(f32[12,28,28,256]{3,0,2,1:T(8,128)} %fusion.15, bf16[12,28,28,512]{3,0,2,1:T(8,128)(2,1)} %all-gather.5.cloned.1.call-done, bf16[1,256,512]{2,1,0:T(8,128)(2,1)S(1)} %copy-done.2), kind=kOutput, calls=%fused_computation.11 | convolution fusion | flops 2471067648 | bytes 24346624 | tf_op jit(solution)/shard_map/nhwo,co->nhwc/dot_general | solution.py:40
  578.2 1.3 collective-permute-start.1
  579.5 7.2 copy.73
  586.7 114.2 %collective-permute-done.1 = bf16[12,28,28,256]{3,2,1,0:T(8,128)(2,1)S(1)} collective-permute-done((bf16[12,28,28,256]{3,2,1,0:T(8,128)(2,1)}, bf16[12,28,28,256]{3,2,1,0:T(8,128)(2,1)S(1)}, u32[]{:S(2)}, u32[]{:S(2)}) %collective-permute-start.1) | collective-permute-done | bytes 4816928 | tf_op jit(solution)/shard_map/ppermute | solution.py:45
  700.9 9.3 %all_to_all.34 = bf16[12,28,28,256]{3,2,1,0:T(8,128)(2,1)} all-to-all(bf16[12,28,28,256]{3,2,1,0:T(8,128)(2,1)S(1)} %collective-permute-done.1), channel_id=1, replica_groups=mesh['dp'=2,'stage'=2,'tp'=2] {'tp'}, dimensions={0} | all-to-all | bytes 9633792 | tf_op jit(solution)/shard_map/all_to_all | solution.py:46
  710.3 14.5 %copy.69 = bf16[6,28,28,2,256]{4,3,2,1,0:T(2,128)(2,1)} copy(bf16[6,28,28,2,256]{4,2,1,0,3:T(8,128)(2,1)} %bitcast.48) | data formatting | bytes 9633792 | tf_op jit(solution)/shard_map/all_to_all | solution.py:46
  724.8 11.7 %broadcast_in_dim.16 = bf16[1,6,28,28,512]{4,3,2,1,0:T(8,128)(2,1)} reshape(bf16[6,28,28,2,256]{4,3,2,1,0:T(2,128)(2,1)} %copy.69) | data formatting | bytes 9633792 | tf_op jit(solution)/shard_map/broadcast_in_dim | solution.py:47
  736.4 0.0 all-reduce.3.cloned.1.call-done
  736.4 2.0 copy.74
  738.5 5.0 copy.103
Async XLA Ops:
  7.2 341.4 %copy-start = (bf16[1,3,3,256,512]{4,3,2,1,0:T(8,128)(2,1)S(1)}, bf16[1,3,3,256,512]{4,3,2,1,0:T(8,128)(2,1)}, u32[]{:S(2)}) copy-start(bf16[1,3,3,256,512]{4,3,2,1,0:T(8,128)(2,1)} %param.8) | copy-start | bytes 7077892
  7.2 376.4 %reduce-scatter.5.cloned.1.call-start = ((), (), s32[]{:S(2)}) async-start(), calls=%async_computation.5 | async-start | bytes 38535168 | tf_op jit(solution)/shard_map/reduce_scatter | solution.py:32
  199.9 126.6 %copy-start.1 = (bf16[1,256,512]{2,1,0:T(8,128)(2,1)S(1)}, bf16[1,256,512]{2,1,0:T(8,128)(2,1)}, u32[]{:S(2)}) copy-start(bf16[1,256,512]{2,1,0:T(8,128)(2,1)} %param.9) | copy-start | bytes 786436
  203.5 123.1 %collective-permute-start = (bf16[12,28,28,256]{3,2,1,0:T(8,128)(2,1)S(1)}, bf16[12,28,28,256]{3,2,1,0:T(8,128)(2,1)}, u32[]{:S(2)}, u32[]{:S(2)}) collective-permute-start(bf16[12,28,28,256]{3,2,1,0:T(8,128)(2,1)S(1)} %bitcast.50), channel_id=1, source_target_pairs={{0,2},{1,3},{4,6},{5,7}} | collective-permute-start | bytes 14450696 | tf_op jit(solution)/shard_map/ppermute | solution.py:24
  348.5 64.4 %reduce-scatter.3.cloned.1.call-start = ((), (), s32[]{:S(2)}) async-start(), calls=%async_computation.4 | async-start | bytes 38535168 | tf_op jit(solution)/shard_map/reduce_scatter | solution.py:32
  383.5 29.4 %copy-start.3 = (f32[1,256]{1,0:T(1,128)S(1)}, f32[1,256]{1,0:T(1,128)}, u32[]{:S(2)}) copy-start(f32[1,256]{1,0:T(1,128)} %param.10) | copy-start | bytes 3076
  383.5 29.4 %copy-start.4 = (f32[1,256]{1,0:T(1,128)S(1)}, f32[1,256]{1,0:T(1,128)}, u32[]{:S(2)}) copy-start(f32[1,256]{1,0:T(1,128)} %param.12) | copy-start | bytes 3076
  383.5 29.4 %copy-start.5 = (f32[1,256]{1,0:T(1,128)S(1)}, f32[1,256]{1,0:T(1,128)}, u32[]{:S(2)}) copy-start(f32[1,256]{1,0:T(1,128)} %param.11) | copy-start | bytes 3076
  383.5 70.9 %all-gather.5.cloned.1.call-start = ((), (), s32[]{:S(2)}) async-start(), calls=%async_computation.7 | async-start | bytes 19267584 | tf_op jit(solution)/shard_map/all_gather | solution.py:39
  430.1 50.0 %all-gather.3.cloned.1.call-start = ((), (), s32[]{:S(2)}) async-start(), calls=%async_computation.6 | async-start | bytes 19267584 | tf_op jit(solution)/shard_map/all_gather | solution.py:39
  444.9 291.6 %all-reduce.3.cloned.1.call-start = ((), (), s32[]{:S(2)}) async-start(), calls=%async_computation.8 | async-start | bytes 10485760 | tf_op jit(solution)/shard_map/psum | solution.py:44
  516.1 35.4 %copy-start.2 = (bf16[1,256,512]{2,1,0:T(8,128)(2,1)S(1)}, bf16[1,256,512]{2,1,0:T(8,128)(2,1)}, u32[]{:S(2)}) copy-start(bf16[1,256,512]{2,1,0:T(8,128)(2,1)} %param.9) | copy-start | bytes 786436
  578.2 122.7 %collective-permute-start.1 = (bf16[12,28,28,256]{3,2,1,0:T(8,128)(2,1)}, bf16[12,28,28,256]{3,2,1,0:T(8,128)(2,1)S(1)}, u32[]{:S(2)}, u32[]{:S(2)}) collective-permute-start(bf16[12,28,28,256]{3,2,1,0:T(8,128)(2,1)} %fusion.6), channel_id=1, source_target_pairs={{2,0},{3,1},{6,4},{7,5}} | collective-permute-start | bytes 14450696 | tf_op jit(solution)/shard_map/ppermute | solution.py:45
Sparse Core Ops, SparseCore 0:
  348.6 29.1 reduce-scatter.4
  383.7 29.1 reduce-scatter.2
  430.2 24.1 all-gather.4
  455.8 24.2 all-gather.2
  516.2 125.9 all-reduce.2
where the time goes:
time: 764 us; the launch traced here: 750 us
  waiting for transfers between devices  281 us (37%)
  local copies, waits for them, and re-layouts  241 us (32%)
  matrix products  151 us (20%)
  other arithmetic  31.9 us (4%)
  blocking collectives  22.2 us (3%)
  between operations  14.3 us (2%)
  starting transfers between devices  9.05 us (1%)
    unnamed x19, local copies, waits for them, and re-layouts  155 us
    ppermute x1, waiting for transfers between devices, device_step(): act_local = lax.ppermute(by_channel, 'stage', perm=[(0, 1)])  116 us
    ppermute x1, waiting for transfers between devices, device_step(): returned = lax.ppermute(grad_local, 'stage', perm=[(1, 0)])  114 us
    conv_general_dilated x2, matrix products, conv_same(): lax.conv_general_dilated(left_op, right_op, (1, 1), 'SAME', dimension_num...  70.4 us
    all_to_all x2, local copies, waits for them, and re-layouts, device_step(): by_channel = lax.all_to_all(act_in[0], 'tp', 3, 0, tiled=True)  42.6 us
    conv_general_dilated x1, matrix products, weight_grad(): lax.conv_general_dilated(images_in, grads_out, (1, 1), ((1, 1), (1, 1)),...  35.9 us
    reduce_scatter x2, waiting for transfers between devices, device_step(): lax.psum_scatter((pre_part, short_part), 'tp', scatter_dimension=3, tiled...  29.3 us
    dot_general x1, matrix products, device_step(): jnp.einsum('nhwo,co->nhwc', g_short_all, short_w, preferred_element_type=...  26.7 us
  transfers between devices with their start and end apart: 7, of which 5 were waited for; matrix products, arithmetic and copies ran while one was open for 21% of the time, Pallas kernels for 0%

commit v1 on v0

v1 whole, which is shorter than its diff:
```python
import functools

import jax
import jax.numpy as jnp
from jax import lax
from jax.experimental import pallas as pl
from jax.experimental.pallas import tpu as pltpu
from jax.sharding import PartitionSpec as P

MESH = pl.DeviceIdType.MESH
F32, BF16 = jnp.float32, jnp.bfloat16
NI = 6
PITCH = 32
ROWS = 28 * PITCH
HALO = PITCH
C = 512
HC = 256
CH = 448
EC = 128
NMSG = 10
DETOUR = (0, 2, 4, 6)
DIRECT = (1, 3, 5, 7, 8, 9)


def rcopy(src, dst, send, recv, dev):
    return pltpu.make_async_remote_copy(src_ref=src, dst_ref=dst, send_sem=send, recv_sem=recv, device_id=dev, device_id_type=MESH)


def dot(a, b):
    return jnp.dot(a, b, preferred_element_type=F32)


def body(x_in, dz_in, w_in, ws_in, vec_in, z_out, dx_out, dw_out,
         xr, dzv, wc, wt, sw, st, acc, tpr, dpr, xcat, gcat, gs, xt, vec,
         xs, xrv, dzl, dzs, dzr, wl, wsd, wr, vl, vs, vr, zl, zs, zr,
         dxs, dxr, ts, tr, ys, yr, ras, rar, rbs, rbr, ol):
    tp = lax.axis_index("tp")
    stage = lax.axis_index("stage")
    dp = lax.axis_index("dp")
    p_x = {"stage": 1 - stage}
    p_t = {"tp": 1 - tp}
    p_d = {"dp": 1 - dp}

    barrier = pltpu.get_barrier_semaphore()
    for dev in (p_x, p_t, p_d):
        pl.semaphore_signal(barrier, inc=1, device_id=dev, device_id_type=MESH)
    pl.semaphore_wait(barrier, 3)

    def x_copy(k):
        return rcopy(x_in.at[k], xr.at[k], xs.at[k], xrv.at[k], p_x)

    def dx_copy(k):
        return rcopy(xr.at[k], dx_out.at[k], dxs.at[k], dxr.at[k], p_x)

    def relay_a(n):
        m = DETOUR[n]
        return rcopy(acc.at[m, pl.ds(pl.multiple_of(tp * HC, HC), HC)], tpr.at[n], ys.at[m], rar.at[n], p_x)

    def relay_b(n):
        return rcopy(tpr.at[n], dpr.at[n], ras.at[n], rbr.at[n], p_d)

    def relay_c(n):
        m = DETOUR[n]
        return rcopy(dpr.at[n], dpr.at[m], rbs.at[n], yr.at[m], p_x)

    @pl.when(stage == 0)
    def _():
        x_copy(0).start()
        x_copy(1).start()
        for k in range(2, NI):
            x_copy(k - 2).wait_send()
            x_copy(k).start()
        x_copy(NI - 2).wait_send()
        x_copy(NI - 1).wait_send()
        nd = len(DETOUR)
        for n in range(nd + 1):
            if n < nd:
                relay_a(n).wait_recv()
                relay_b(n).start()
            if n > 0:
                relay_b(n - 1).wait_recv()
                relay_c(n - 1).start()
        for n in range(nd):
            relay_b(n).wait_send()
            relay_c(n).wait_send()
        for k in range(NI):
            dx_copy(k).wait_recv()

    @pl.when(stage == 1)
    def _():
        lanes = pl.ds(pl.multiple_of(tp * HC, HC), HC)
        other = pl.ds(pl.multiple_of((1 - tp) * HC, HC), HC)

        def dz_local(k):
            return pltpu.make_async_copy(dz_in.at[tp * NI + k], dzv.at[k, :, lanes], dzl.at[k])

        def dz_remote(k):
            return rcopy(dz_in.at[(1 - tp) * NI + k], dzv.at[k, :, lanes], dzs.at[k], dzr.at[k], p_t)

        def w_dst(m):
            if m == 9:
                return sw.at[lanes]
            i, j = divmod(m, 3)
            return wc.at[i, pl.ds(pl.multiple_of(j * C + tp * HC, HC), HC)]

        def w_src(m):
            return ws_in if m == 9 else w_in.at[m]

        def w_local(m):
            return pltpu.make_async_copy(w_src(m), w_dst(m), wl.at[m])

        def w_remote(m):
            return rcopy(w_src(m), w_dst(m), wsd.at[m], wr.at[m], p_t)

        def v_local():
            return pltpu.make_async_copy(vec_in, vec.at[:, lanes], vl.at[0])

        def v_remote():
            return rcopy(vec_in, vec.at[:, lanes], vs.at[0], vr.at[0], p_t)

        def z_local(k):
            return pltpu.make_async_copy(dzv.at[k, :, lanes], z_out.at[tp * NI + k], zl.at[k])

        def z_remote(k):
            return rcopy(dzv.at[k, :, other], z_out.at[tp * NI + k], zs.at[k], zr.at[k], p_t)

        def t_copy(m):
            return rcopy(acc.at[m, other], tpr.at[m], ts.at[m], tr.at[m], p_t)

        def y_copy(m):
            return rcopy(acc.at[m, lanes], dpr.at[m], ys.at[m], yr.at[m], p_d)

        def out_copy(m):
            return pltpu.make_async_copy(tpr.at[m], dw_out.at[m], ol.at[m])

        for m in range(NMSG):
            w_local(m).start()
            w_remote(m).start()
        v_local().start()
        v_remote().start()

        @pl.loop(0, NI)
        def _(k):
            dz_local(k).start()
            dz_remote(k).start()

        @pl.loop(0, NMSG)
        def _(m):
            acc[m] = jnp.zeros((C, C), F32)

        for ref in (xcat, gcat):
            ref[0:HALO] = jnp.zeros((HALO, 3 * C), BF16)
            ref[HALO + ROWS:] = jnp.zeros((HALO, 3 * C), BF16)
        for m in range(NMSG):
            w_local(m).wait()
            w_remote(m).wait()
        v_local().wait()
        v_remote().wait()
        st[...] = sw[...].T

        @pl.loop(0, 3)
        def _(i):
            for j in range(3):
                wt[i, j * C:(j + 1) * C] = wc[i, j * C:(j + 1) * C].T

        @pl.loop(0, NI)
        def _(k):
            x_copy(k).wait_recv()
            for e in range(ROWS // EC):
                xv = xr[k, e * EC:(e + 1) * EC]
                xf = xv.astype(F32)
                dst = slice(HALO + e * EC, HALO + (e + 1) * EC)
                xcat[dst, C:2 * C] = xv
                xcat[dst, 0:C] = pltpu.roll(xf, 1, 0).astype(BF16)
                xcat[dst, 2 * C:] = pltpu.roll(xf, EC - 1, 0).astype(BF16)
            dz_local(k).wait()
            dz_remote(k).wait()
            for r in range(0, ROWS, CH):
                pre = dot(xcat[r:r + CH], wc[0]) + dot(xcat[r + HALO:r + HALO + CH], wc[1]) + dot(xcat[r + 2 * HALO:r + 2 * HALO + CH], wc[2])
                short = dot(xcat[r + HALO:r + HALO + CH, C:2 * C], sw[...])
                u = pre * vec[0:1] + vec[1:2] + short * vec[2:3]
                dz = dzv[k, r:r + CH].astype(F32)
                dzv[k, r:r + CH] = jnp.maximum(u, 0.0).astype(BF16)
                g = jnp.where(u > 0.0, dz * vec[0:1], 0.0)
                gs[r:r + CH] = jnp.where(u > 0.0, dz * vec[2:3], 0.0).astype(BF16)
                dst = slice(HALO + r, HALO + r + CH)
                gcat[dst, 0:C] = pltpu.roll(g, CH - 1, 0).astype(BF16)
                gcat[dst, C:2 * C] = g.astype(BF16)
                gcat[dst, 2 * C:] = pltpu.roll(g, 1, 0).astype(BF16)
            z_local(k).start()
            z_remote(k).start()

            for i in range(3):
                xt[i] = xcat[i * HALO:i * HALO + ROWS, C:2 * C].T
            for i in range(3):
                for j in range(3):
                    acc[3 * i + j] += dot(xt[i], gcat[HALO:HALO + ROWS, j * C:(j + 1) * C])
            acc[9] += dot(xt[1], gs[...])

            @pl.when(k == NI - 1)
            def _():
                for m in range(NMSG):
                    t_copy(m).start()
                for m in range(NMSG):
                    t_copy(m).wait_recv()
                    acc[m, lanes] = acc[m, lanes] + tpr[m]
                    if m in DETOUR:
                        relay_a(DETOUR.index(m)).start()
                    else:
                        y_copy(m).start()

            for r in range(0, ROWS, CH):
                dx = dot(gcat[r + 2 * HALO:r + 2 * HALO + CH], wt[0]) + dot(gcat[r + HALO:r + HALO + CH], wt[1]) + dot(gcat[r:r + CH], wt[2]) + dot(gs[r:r + CH], st[...])
                xr[k, r:r + CH] = dx.astype(BF16)
            dx_copy(k).start()

        for m in DIRECT + DETOUR:
            y_copy(m).wait_recv()
            tpr[m] = acc[m, lanes] + dpr[m]
            out_copy(m).start()

        @pl.loop(0, NMSG)
        def _(m):
            t_copy(m).wait_send()
            y_copy(m).wait_send()
            out_copy(m).wait()

        @pl.loop(0, NI)
        def _(k):
            z_local(k).wait()
            z_remote(k).wait()
            dx_copy(k).wait_send()


def block(x_pad, dz_pad, w, ws, vecs):
    any_spec = pl.BlockSpec(memory_space=pl.ANY)
    dma = lambda n: pltpu.SemaphoreType.DMA((n,))
    nd = len(DETOUR)
    return pl.pallas_call(
        body,
        out_shape=(
            jax.ShapeDtypeStruct((2 * NI, ROWS, HC), BF16),
            jax.ShapeDtypeStruct((NI, ROWS, C), BF16),
            jax.ShapeDtypeStruct((NMSG, HC, C), F32),
        ),
        in_specs=[any_spec] * 5,
        out_specs=(any_spec,) * 3,
        scratch_shapes=[
            pltpu.VMEM((NI, ROWS, C), BF16),
            pltpu.VMEM((NI, ROWS, C), BF16),
            pltpu.VMEM((3, 3 * C, C), BF16),
            pltpu.VMEM((3, 3 * C, C), BF16),
            pltpu.VMEM((C, C), BF16),
            pltpu.VMEM((C, C), BF16),
            pltpu.VMEM((NMSG, C, C), F32),
            pltpu.VMEM((NMSG, HC, C), F32),
            pltpu.VMEM((NMSG, HC, C), F32),
            pltpu.VMEM((ROWS + 2 * HALO, 3 * C), BF16),
            pltpu.VMEM((ROWS + 2 * HALO, 3 * C), BF16),
            pltpu.VMEM((ROWS, C), BF16),
            pltpu.VMEM((3, C, ROWS), BF16),
            pltpu.VMEM((8, C), F32),
            dma(NI), dma(NI), dma(NI), dma(NI), dma(NI), dma(NMSG), dma(NMSG), dma(NMSG), dma(1), dma(1), dma(1), dma(NI), dma(NI), dma(NI),
            dma(NI), dma(NI), dma(NMSG), dma(NMSG), dma(NMSG), dma(NMSG), dma(nd), dma(nd), dma(nd), dma(nd), dma(NMSG),
        ],
        compiler_params=pltpu.CompilerParams(collective_id=0, has_side_effects=True, vmem_limit_bytes=67043328),
        name="conv_block",
    )(x_pad, dz_pad, w, ws, vecs)


def solution(mesh):
    act_spec = P("stage", ("dp", "tp"), None, None, None)
    kernel_spec = P("stage", None, None, "tp", None)
    short_spec = P("stage", "tp", None)
    vec_spec = P("stage", "tp")
    grad_spec = P("stage", "dp", None, None, "tp")

    def device_step(act_in, w_conv, w_short, gamma, beta, gamma_s, grad_z):
        stage = lax.axis_index("stage")
        widen = lambda a: jnp.pad(a, ((0, 0), (0, 0), (0, PITCH - 28), (0, 0))).reshape(a.shape[0], ROWS, a.shape[3])
        narrow = lambda a: a.reshape(a.shape[0], 28, PITCH, a.shape[2])[:, :, :28]
        vecs = jnp.concatenate([gamma, beta, gamma_s, jnp.zeros((5, HC), F32)], axis=0)
        z, dx, dw = block(widen(act_in[0]), widen(grad_z[0]), w_conv.reshape(9, HC, C), w_short[0], vecs)
        z = jnp.where(stage == 1, narrow(z), jnp.zeros((), BF16))
        dx = jnp.where(stage == 0, narrow(dx), jnp.zeros((), BF16))
        dw = jnp.where(stage == 1, dw, 0.0)
        return z[None], dx[None], dw[:9].reshape(1, 3, 3, HC, C), dw[9][None]

    return jax.shard_map(device_step, mesh=mesh, in_specs=(act_spec, kernel_spec, short_spec, vec_spec, vec_spec, vec_spec, grad_spec), out_specs=(grad_spec, act_spec, kernel_spec, short_spec), check_vma=False)
```

time: 764 us -> 234 us (0.31)
  the two profiles are of different devices: /device:TPU:0 before, /device:TPU:3 now
where the time goes in v1:
time: 234 us
  Pallas kernels  207 us (88%)
  local copies, waits for them, and re-layouts  13.4 us (6%)
  other arithmetic  12.1 us (5%)
    pallas_call x1, Pallas kernels, block(): pl.pallas_call(body, out_shape=(jax.ShapeDtypeStruct((2 * NI, ROWS, HC),...  207 us
    pad x2, local copies, waits for them, and re-layouts, device_step(): jnp.pad(a, ((0, 0), (0, 0), (0, PITCH - 28), (0, 0)))  9.67 us
    broadcast_in_dim x2, other arithmetic, device_step(): return (z[None], dx[None], dw[:9].reshape(1, 3, 3, HC, C), dw[9][None])  8.16 us

profile of v1, /device:TPU:3, one launch (start us, length us, event | category | flops | bytes accessed | tf_op | source)
XLA Modules:
  0.0 233.6 jit_solution(17918272661600807351)
XLA Ops:
  0.6 0.0 copy-start
  0.6 6.3 %pad.8 = bf16[6,28,32,512]{3,2,1,0:T(8,128)(2,1)} pad(bf16[6,28,28,512]{3,2,1,0:T(8,128)(2,1)} %bitcast.15, bf16[]{:T(256)} %constant.4.clone.1), padding=0_0x0_0x0_4x0_0 | pad | bytes 10321922 | tf_op jit(solution)/shard_map/jit(_pad)/pad | solution.py:280
  7.0 0.0 copy-done
  7.0 0.0 copy-start.1
  7.0 0.0 copy-start.2
  7.0 0.0 copy-start.3
  7.0 3.4 %pad.9 = bf16[12,28,32,256]{3,2,1,0:T(8,128)(2,1)} pad(bf16[12,28,28,256]{3,2,1,0:T(8,128)(2,1)S(1)} %bitcast.16, bf16[]{:T(256)} %constant.4.clone.1), padding=0_0x0_0x0_4x0_0 | pad | bytes 10321922 | tf_op jit(solution)/shard_map/jit(_pad)/pad | solution.py:280
  10.3 0.1 pad.13.clone
  10.4 0.0 copy-done.1
  10.4 0.0 copy-done.2
  10.4 0.0 copy-done.3
  10.4 0.7 maximum_maximum_fusion.vec_in
  11.1 207.4 %conv_block.1 = (bf16[12,896,256]{2,1,0:T(8,128)(2,1)}, bf16[6,896,512]{2,1,0:T(8,128)(2,1)}, f32[10,256,512]{2,1,0:T(8,128)}) custom-call(bf16[6,896,512]{2,1,0:T(8,128)(2,1)} %bitcast.13, bf16[12,896,256]{2,1,0:T(8,128)(2,1)} %bitcast.14, bf16[9,256,512]{2,1,0:T(8,128)(2,1)} %bitcast.22, bf16[256,512]{1,0:T(8,128)(2,1)} %bitcast.23, ...), custom_call_target="tpu_custom_call" | custom-call | tf_op jit(solution)/shard_map/conv_block/pallas_call | solution.py:239
  218.5 0.0 slice-start
  218.5 3.3 %broadcast_select_fusion = f32[10,256,512]{2,1,0:T(8,128)S(1)} fusion(f32[10,256,512]{2,1,0:T(8,128)} %get-tuple-element.9, pred[]{:T(512)S(6)} %eq.7), kind=kLoop, calls=%fused_computation.4 | loop fusion | flops 1310720 | bytes 10485761 | tf_op jit(solution)/shard_map/jit(_where)/select_n | solution.py:286
  221.8 0.0 slice-start.1
  221.8 2.8 %slice.18 = f32[9,256,512]{2,1,0:T(8,128)} slice(f32[10,256,512]{2,1,0:T(8,128)S(1)} %broadcast_select_fusion), slice={[0:9], [0:256], [0:512]} | slice | bytes 9437184 | tf_op jit(solution)/shard_map/slice | solution.py:287
  224.6 0.8 slice.19
  225.4 0.0 slice-done
  225.4 0.0 slice-done.1
  225.4 2.8 %fusion.1 = bf16[1,12,28,28,256]{4,3,2,1,0:T(8,128)(2,1)} fusion(bf16[12,28,32,256]{3,2,1,0:T(8,128)(2,1)S(1)} %bitcast.20, pred[]{:T(512)S(6)} %eq.7), kind=kLoop, calls=%fused_computation.3 | loop fusion | flops 2408448 | bytes 9633793 | tf_op jit(solution)/shard_map/broadcast_in_dim | solution.py:287
  228.2 5.4 %fusion = bf16[1,6,28,28,512]{4,3,2,1,0:T(8,128)(2,1)} fusion(bf16[6,28,32,512]{3,2,1,0:T(8,128)(2,1)} %bitcast.17, pred[]{:T(512)S(6)} %eq.8), kind=kLoop, calls=%fused_computation.1 | loop fusion | flops 2408448 | bytes 9633793 | tf_op jit(solution)/shard_map/broadcast_in_dim | solution.py:287
  (2 shorter events, 0.0 us)
Async XLA Ops:
  0.6 6.3 %copy-start = (bf16[1,12,28,28,256]{4,3,2,1,0:T(8,128)(2,1)S(1)}, bf16[1,12,28,28,256]{4,3,2,1,0:T(8,128)(2,1)}, u32[]{:S(2)}) copy-start(bf16[1,12,28,28,256]{4,3,2,1,0:T(8,128)(2,1)} %param.13) | copy-start | bytes 14450692
  7.0 3.4 %copy-start.1 = (f32[1,256]{1,0:T(1,128)S(1)}, f32[1,256]{1,0:T(1,128)}, u32[]{:S(2)}) copy-start(f32[1,256]{1,0:T(1,128)} %param.12) | copy-start | bytes 3076
  7.0 3.4 %copy-start.2 = (f32[1,256]{1,0:T(1,128)S(1)}, f32[1,256]{1,0:T(1,128)}, u32[]{:S(2)}) copy-start(f32[1,256]{1,0:T(1,128)} %param.11) | copy-start | bytes 3076
  7.0 3.4 %copy-start.3 = (f32[1,256]{1,0:T(1,128)S(1)}, f32[1,256]{1,0:T(1,128)}, u32[]{:S(2)}) copy-start(f32[1,256]{1,0:T(1,128)} %param.10) | copy-start | bytes 3076
  218.5 6.9 %slice-start = ((s8[5505024]{0:T(1024)(128)(4,1)}), s8[4194304]{0:T(1024)(128)(4,1)S(1)}, s32[]{:S(2)}) async-start(s8[5505024]{0:T(1024)(128)(4,1)} %bitcast.18), calls=%async_computation | async-start | bytes 8388608
  221.8 3.6 %slice-start.1 = ((s8[5505024]{0:T(1024)(128)(4,1)}), s8[1310720]{0:T(1024)(128)(4,1)S(1)}, s32[]{:S(2)}) async-start(s8[5505024]{0:T(1024)(128)(4,1)} %bitcast.18), calls=%async_computation.1 | async-start | bytes 2621440

commit v2 on v0

v2 whole, which is shorter than its diff:
```python
import jax
import jax.numpy as jnp
from jax import lax
from jax.experimental import pallas as pl
from jax.experimental.pallas import tpu as pltpu
from jax.sharding import PartitionSpec as P

MESH = pl.DeviceIdType.MESH
F32, BF16 = jnp.float32, jnp.bfloat16
NI = 6
SIDE = 28
PITCH = 32
ROWS = SIDE * PITCH
PIX = SIDE * SIDE
HALO = PITCH
C = 512
HC = 256
BLK, PBLK = 4 * PITCH, 4 * SIDE
CHUNKS = ((0, 512), (512, 384))
DXCHUNKS = ((0, 384), (384, 512))
NTAP = 10
UNIT = 64
NU = HC // UNIT
RELAYED = tuple((m, s) for m in range(9) for s in range(2))[:18]
STRAIGHT = tuple((m, s) for m in range(NTAP) for s in range(NU) if (m, s) not in RELAYED)
ARRIVAL = sorted([(i + 1, u) for i, u in enumerate(STRAIGHT)] + [(i + 5.5, u) for i, u in enumerate(RELAYED)])
SPLIT = 5


def rcopy(src, dst, send, recv, dev):
    return pltpu.make_async_remote_copy(src_ref=src, dst_ref=dst, send_sem=send, recv_sem=recv, device_id=dev, device_id_type=MESH)


def dot(a, b):
    return jnp.dot(a, b, preferred_element_type=F32)


def body(x_in, dz_in, w_in, ws_in, gam_in, bet_in, gas_in, z_out, dx_out, dw_out, ds_out,
         xr, dzv, wc, wt, sw, st, acc, tpr, dpr, xcat, gcat, gs, xt, gam, bet, gas, xraw, dzraw, dzt, widen, pack,
         xs, xrv, xl, dzl, dzs, dzr, wl, wsd, wr, vl, vs, vr, zl, zs, zr,
         dxs, dxr, dxo, ts, tr, ys, yr, ras, rar, rbs, rbr, ol):
    tp = lax.axis_index("tp")
    stage = lax.axis_index("stage")
    p_x = {"stage": 1 - stage}
    p_t = {"tp": 1 - tp}
    p_d = {"dp": 1 - lax.axis_index("dp")}

    def load_part(k):
        x_load(k).wait()
        for h in range(SIDE):
            gs[h * PITCH:h * PITCH + SIDE] = xraw[k % 2, h]
        if k + 2 < NI:
            x_load(k + 2).start()

    def pack_part(k, p):
        for b in range(SPLIT) if p == 0 else range(SPLIT, SIDE // 4):
            xr[k, b * PBLK:(b + 1) * PBLK] = dot(pack[...], gs[b * BLK:(b + 1) * BLK]).astype(BF16)

    barrier = pltpu.get_barrier_semaphore()
    for dev in (p_x, p_t, p_d):
        pl.semaphore_signal(barrier, inc=1, device_id=dev, device_id_type=MESH)

    def select(shape, padded_axis):
        wide = lax.broadcasted_iota(jnp.int32, shape, padded_axis)
        slim = lax.broadcasted_iota(jnp.int32, shape, 1 - padded_axis)
        col = wide & (PITCH - 1)
        hit = (slim == (wide >> 5) * SIDE + col) & (col < SIDE)
        return jnp.where(hit, 1.0, 0.0).astype(BF16)


    def x_copy(k, p):
        at = slice(0, SPLIT * PBLK) if p == 0 else slice(SPLIT * PBLK, PIX)
        return rcopy(xr.at[k, at], xr.at[k, at], xs.at[k, p], xrv.at[k, p], p_x)

    def x_load(k):
        return pltpu.make_async_copy(x_in.at[k], xraw.at[k % 2], xl.at[k])

    def dx_copy(k, c, h):
        r, n = DXCHUNKS[c]
        at = slice(r // PITCH * SIDE, (r + n) // PITCH * SIDE)
        return rcopy(xr.at[k, at, h * HC:(h + 1) * HC], dzv.at[k, h, at], dxs.at[k, c, h], dxr.at[k, c, h], p_x)

    def unit_rows(u):
        return pl.ds(pl.multiple_of(tp * HC + u[1] * UNIT, UNIT), UNIT)

    def part(ref, u):
        return ref.at[u[0], u[1] * UNIT:(u[1] + 1) * UNIT]

    def held(ref, n):
        return part(ref, divmod(n, NU))

    def relay_a(n):
        m, s = RELAYED[n]
        return rcopy(acc.at[m, unit_rows((m, s))], held(tpr, n), ys.at[m, s], rar.at[n], p_x)

    def relay_b(n):
        return rcopy(held(tpr, n), held(dpr, n), ras.at[n], rbr.at[n], p_d)

    def relay_c(n):
        m, s = RELAYED[n]
        return rcopy(held(dpr, n), part(dpr, (m, s)), rbs.at[n], yr.at[m, s], p_x)

    widen[...] = select((BLK, PBLK), 0)
    pack[...] = select((PBLK, BLK), 1)

    @pl.when(stage == 0)
    def _():
        x_load(0).start()
        x_load(1).start()
        gs[...] = jnp.zeros((ROWS, C), BF16)
        load_part(0)
        pack_part(0, 0)
        pack_part(0, 1)

    pl.semaphore_wait(barrier, 3)

    @pl.when(stage == 0)
    def _():
        def dx_store(k):
            return pltpu.make_async_copy(xraw.at[k % 2], dx_out.at[k], dxo.at[k])

        x_copy(0, 0).start()
        x_copy(0, 1).start()
        for k in range(1, NI):
            load_part(k)
            pack_part(k, 0)
            if k > 1:
                x_copy(k - 2, 0).wait_send()
                x_copy(k - 2, 1).wait_send()
            x_copy(k, 0).start()
            pack_part(k, 1)
            x_copy(k, 1).start()
        for k in range(NI - 2, NI):
            x_copy(k, 0).wait_send()
            x_copy(k, 1).wait_send()

        def take_dx(k):
            for c in range(2):
                for h in range(2):
                    dx_copy(k, c, h).wait_recv()
            if k > 1:
                dx_store(k - 2).wait()
            for b in range(SIDE // 4):
                for h in range(2):
                    wide = dot(widen[...], dzv[k, h, b * PBLK:(b + 1) * PBLK]).astype(BF16)
                    for r in range(4):
                        xraw[k % 2, 4 * b + r, :, h * HC:(h + 1) * HC] = wide[r * PITCH:r * PITCH + SIDE]
            dx_store(k).start()

        for k in range(NI - 1):
            take_dx(k)
        nr = len(RELAYED)
        for n in range(nr + 1):
            if n < nr:
                relay_a(n).wait_recv()
                relay_b(n).start()
            if n > 0:
                relay_b(n - 1).wait_recv()
                relay_c(n - 1).start()
        take_dx(NI - 1)
        for n in range(nr):
            relay_b(n).wait_send()
            relay_c(n).wait_send()
        dx_store(NI - 2).wait()
        dx_store(NI - 1).wait()

    @pl.when(stage == 1)
    def _():
        lanes = pl.ds(pl.multiple_of(tp * HC, HC), HC)
        other = pl.ds(pl.multiple_of((1 - tp) * HC, HC), HC)

        def dz_load(k, q):
            img = (tp if q == 0 else 1 - tp) * NI + k
            return pltpu.make_async_copy(dz_in.at[img], dzraw.at[lax.rem(k, 2), q], dzl.at[k, q])

        def dz_send(k):
            return rcopy(dzt.at[lax.rem(k, 2)], dzv.at[k, tp], dzs.at[k], dzr.at[k], p_t)

        def w_dst(m):
            if m == 9:
                return sw.at[lanes]
            i, j = divmod(m, 3)
            return wc.at[i, pl.ds(pl.multiple_of(j * C + tp * HC, HC), HC)]

        def w_src(m):
            return ws_in if m == 9 else w_in.at[m]

        def w_local(m):
            return pltpu.make_async_copy(w_src(m), w_dst(m), wl.at[m])

        def w_remote(m):
            return rcopy(w_src(m), w_dst(m), wsd.at[m], wr.at[m], p_t)

        vecs = ((gam_in, gam), (bet_in, bet), (gas_in, gas))

        def v_local(i):
            return pltpu.make_async_copy(vecs[i][0], vecs[i][1].at[:, lanes], vl.at[i])

        def v_remote(i):
            return rcopy(vecs[i][0], vecs[i][1].at[:, lanes], vs.at[i], vr.at[i], p_t)

        def z_local(k):
            return pltpu.make_async_copy(dzraw.at[lax.rem(k, 2), tp], z_out.at[tp * NI + k], zl.at[k])

        def z_remote(k):
            return rcopy(dzraw.at[lax.rem(k, 2), 1 - tp], z_out.at[tp * NI + k], zs.at[k], zr.at[k], p_t)

        def t_copy(m):
            return rcopy(acc.at[m, other], tpr.at[m], ts.at[m], tr.at[m], p_t)

        def y_copy(u):
            return rcopy(acc.at[u[0], unit_rows(u)], part(dpr, u), ys.at[u[0], u[1]], yr.at[u[0], u[1]], p_d)

        def out_copy(u):
            m, s = u
            rows = slice(s * UNIT, (s + 1) * UNIT)
            dst = ds_out.at[rows] if m == 9 else dw_out.at[m, rows]
            return pltpu.make_async_copy(part(tpr, u), dst, ol.at[m, s])

        for k in range(2):
            for q in range(2):
                dz_load(k, q).start()
        for m in range(NTAP):
            w_local(m).start()
            w_remote(m).start()
        for i in range(3):
            v_local(i).start()
            v_remote(i).start()

        zero = jnp.zeros((ROWS, HC), BF16)
        for q in range(2):
            dzt[q] = zero

        @pl.loop(0, NI)
        def _(k):
            dzv[k, tp] = zero
            for q in range(2):
                dz_load(k, q).wait()

            @pl.when(k >= 2)
            def _():
                dz_send(k - 2).wait_send()

            slot = lax.rem(k, 2)
            for h in range(SIDE):
                dzv[k, tp, h * PITCH:h * PITCH + SIDE] = dzraw[slot, 0, h]
                dzt[slot, h * PITCH:h * PITCH + SIDE] = dzraw[slot, 1, h]
            dz_send(k).start()

            @pl.when(k < NI - 2)
            def _():
                for q in range(2):
                    dz_load(k + 2, q).start()

        @pl.loop(0, NTAP)
        def _(m):
            acc[m] = jnp.zeros((C, C), F32)

        for ref in (xcat, gcat):
            ref[0:HALO] = jnp.zeros((HALO, 3 * C), BF16)
            ref[HALO + ROWS:] = jnp.zeros((HALO, 3 * C), BF16)
        for m in range(NTAP):
            w_local(m).wait()
            w_remote(m).wait()
        for i in range(3):
            v_local(i).wait()
            v_remote(i).wait()
        st[...] = sw[...].T

        @pl.loop(0, 3)
        def _(i):
            for j in range(3):
                wt[i, j * C:(j + 1) * C] = wc[i, j * C:(j + 1) * C].T

        @pl.loop(0, 2)
        def _(k):
            dz_send(NI - 2 + k).wait_send()

        def pass_on(m):
            t_copy(m).wait_recv()
            for s in range(NU):
                u = (m, s)
                rows = unit_rows(u)
                acc[m, rows] = acc[m, rows] + tpr[m, s * UNIT:(s + 1) * UNIT]
                if u in RELAYED:
                    relay_a(RELAYED.index(u)).start()
                else:
                    y_copy(u).start()

        def forward(k, blocks, r, n):
            for b in blocks:
                xf = dot(widen[...], xr[k, b * PBLK:(b + 1) * PBLK])
                dst = slice(HALO + b * BLK, HALO + (b + 1) * BLK)
                xcat[dst, C:2 * C] = xf.astype(BF16)
                xcat[dst, 0:C] = pltpu.roll(xf, 1, 0).astype(BF16)
                xcat[dst, 2 * C:] = pltpu.roll(xf, BLK - 1, 0).astype(BF16)
            pre = dot(xcat[r:r + n], wc[0]) + dot(xcat[r + HALO:r + HALO + n], wc[1]) + dot(xcat[r + 2 * HALO:r + 2 * HALO + n], wc[2])
            short = dot(xcat[r + HALO:r + HALO + n, C:2 * C], sw[...])
            u = pre * gam[...] + bet[...] + short * gas[...]
            z = jnp.maximum(u, 0.0).astype(BF16)
            for h in range(n // PITCH):
                for q in range(2):
                    dzraw[lax.rem(k, 2), q, r // PITCH + h] = z[h * PITCH:h * PITCH + SIDE, q * HC:(q + 1) * HC]
            dz = jnp.concatenate([dzv[k, 0, r:r + n], dzv[k, 1, r:r + n]], axis=1).astype(F32)
            g = jnp.where(u > 0.0, dz * gam[...], 0.0)
            gs[r:r + n] = jnp.where(u > 0.0, dz * gas[...], 0.0).astype(BF16)
            dst = slice(HALO + r, HALO + r + n)
            gcat[dst, 0:C] = pltpu.roll(g, n - 1, 0).astype(BF16)
            gcat[dst, C:2 * C] = g.astype(BF16)
            gcat[dst, 2 * C:] = pltpu.roll(g, 1, 0).astype(BF16)

        def image(k, last):
            def free_slot():
                z_local(k - 2).wait()
                z_remote(k - 2).wait_send()

            free_slot() if last else pl.when(k >= 2)(free_slot)
            dz_send(k).wait_recv()
            x_copy(k, 0).wait_recv()
            forward(k, range(SPLIT), *CHUNKS[0])

            def input_part(c):
                r, n = DXCHUNKS[c]
                dx = dot(gcat[r + 2 * HALO:r + 2 * HALO + n], wt[0]) + dot(gcat[r + HALO:r + HALO + n], wt[1]) + dot(gcat[r:r + n], wt[2]) + dot(gs[r:r + n], st[...])
                dx = dx.astype(BF16)
                for b in range(n // BLK):
                    at = (r // BLK + b) * PBLK
                    xr[k, at:at + PBLK] = dot(pack[...], dx[b * BLK:(b + 1) * BLK]).astype(BF16)
                for h in range(2):
                    dx_copy(k, c, h).start()

            input_part(0)
            x_copy(k, 1).wait_recv()
            forward(k, range(SPLIT, SIDE // 4), *CHUNKS[1])
            z_local(k).start()
            z_remote(k).start()

            def weight_part():
                xt[...] = xcat[HALO:HALO + ROWS, C:2 * C].T
                for m in range(NTAP):
                    if m == 9:
                        acc[9] += dot(xt[...], gs[...])
                    else:
                        i, j = divmod(m, 3)
                        at = (2 - i) * HALO
                        acc[m] += dot(xt[...], gcat[at:at + ROWS, j * C:(j + 1) * C])
                    if last:
                        t_copy(m).start()
                        if m >= 2:
                            pass_on(m - 2)
                if last:
                    pass_on(NTAP - 2)
                    pass_on(NTAP - 1)

            if last:
                weight_part()
                input_part(1)
            else:
                input_part(1)
                weight_part()

        @pl.loop(0, NI - 1)
        def _(k):
            image(k, False)

        image(NI - 1, True)

        for _, u in ARRIVAL:
            y_copy(u).wait_recv()
            m, s = u
            tpr[m, s * UNIT:(s + 1) * UNIT] = acc[m, unit_rows(u)] + part(dpr, u)[...]
            out_copy(u).start()

        for m in range(NTAP):
            t_copy(m).wait_send()
            for s in range(NU):
                y_copy((m, s)).wait_send()
                out_copy((m, s)).wait()

        for k in range(NI - 2, NI):
            z_local(k).wait()
            z_remote(k).wait_send()
        for k in range(NI):
            z_remote(k).wait_recv()
            for c in range(2):
                for h in range(2):
                    dx_copy(k, c, h).wait_send()


def finish_body(z_in, dx_in, dw_in, ds_in, z_out, dx_out, dw_out, ds_out, zb, dxb, dwb, dsb, z0, dx0, dw0, sems):
    stage = lax.axis_index("stage")
    groups = ((z_in, zb, z_out, z0, 2 * NI, 1), (dx_in, dxb, dx_out, dx0, NI, 0), (dw_in, dwb, dw_out, dw0, 9, 1), (ds_in, dsb, ds_out, dw0, 1, 1))

    def run(here):
        def pick(ref, k):
            return ref.at[k] if len(ref.shape) > 2 else ref

        ins, outs, n = [], [], 0
        for src, buf, dst, nil, count, owner in groups:
            for k in range(count):
                if owner == here:
                    ins.append(pltpu.make_async_copy(pick(src, k), pick(buf, k), sems.at[0, n]))
                    outs.append(pltpu.make_async_copy(pick(buf, k), pick(dst, k), sems.at[1, n]))
                else:
                    outs.append(pltpu.make_async_copy(nil, pick(dst, k), sems.at[1, n]))
                    ins.append(None)
                n += 1
        for c in ins:
            if c is not None:
                c.start()
        if here == 0:
            z0[...] = jnp.zeros(z0.shape, z0.dtype)
            dw0[...] = jnp.zeros(dw0.shape, dw0.dtype)
        else:
            dx0[...] = jnp.zeros(dx0.shape, dx0.dtype)
        for c, o in zip(ins, outs):
            if c is None:
                o.start()
        for c, o in zip(ins, outs):
            if c is not None:
                c.wait()
                o.start()
        for o in outs:
            o.wait()

    for here in range(2):
        pl.when(stage == here)(lambda here=here: run(here))


def finish(z, dx, dw, ds):
    any_spec = pl.BlockSpec(memory_space=pl.ANY)
    total = 2 * NI + NI + 9 + 1
    return pl.pallas_call(
        finish_body,
        out_shape=tuple(jax.ShapeDtypeStruct(a.shape, a.dtype) for a in (z, dx, dw, ds)),
        in_specs=[any_spec] * 4,
        out_specs=(any_spec,) * 4,
        scratch_shapes=[pltpu.VMEM(a.shape, a.dtype) for a in (z, dx, dw, ds)]
        + [pltpu.VMEM(z.shape[1:], z.dtype), pltpu.VMEM(dx.shape[1:], dx.dtype), pltpu.VMEM(ds.shape, ds.dtype), pltpu.SemaphoreType.DMA((2, total))],
        compiler_params=pltpu.CompilerParams(vmem_limit_bytes=67043328),
        name="finish",
    )(z, dx, dw, ds)


def block(x, dz, w, ws, gamma, beta, gamma_s):
    any_spec = pl.BlockSpec(memory_space=pl.ANY)
    dma = lambda *n: pltpu.SemaphoreType.DMA(n)
    nr = len(RELAYED)
    return pl.pallas_call(
        body,
        out_shape=(
            jax.ShapeDtypeStruct((2 * NI, SIDE, SIDE, HC), BF16),
            jax.ShapeDtypeStruct((NI, SIDE, SIDE, C), BF16),
            jax.ShapeDtypeStruct((9, HC, C), F32),
            jax.ShapeDtypeStruct((HC, C), F32),
        ),
        in_specs=[any_spec] * 7,
        out_specs=(any_spec,) * 4,
        scratch_shapes=[
            pltpu.VMEM((NI, PIX, C), BF16),
            pltpu.VMEM((NI, 2, ROWS, HC), BF16),
            pltpu.VMEM((3, 3 * C, C), BF16),
            pltpu.VMEM((3, 3 * C, C), BF16),
            pltpu.VMEM((C, C), BF16),
            pltpu.VMEM((C, C), BF16),
            pltpu.VMEM((NTAP, C, C), F32),
            pltpu.VMEM((NTAP, HC, C), F32),
            pltpu.VMEM((NTAP, HC, C), F32),
            pltpu.VMEM((ROWS + 2 * HALO, 3 * C), BF16),
            pltpu.VMEM((ROWS + 2 * HALO, 3 * C), BF16),
            pltpu.VMEM((ROWS, C), BF16),
            pltpu.VMEM((C, ROWS), BF16),
            pltpu.VMEM((1, C), F32),
            pltpu.VMEM((1, C), F32),
            pltpu.VMEM((1, C), F32),
            pltpu.VMEM((2, SIDE, SIDE, C), BF16),
            pltpu.VMEM((2, 2, SIDE, SIDE, HC), BF16),
            pltpu.VMEM((2, ROWS, HC), BF16),
            pltpu.VMEM((BLK, PBLK), BF16),
            pltpu.VMEM((PBLK, BLK), BF16),
            dma(NI, 2), dma(NI, 2), dma(NI), dma(NI, 2), dma(NI), dma(NI), dma(NTAP), dma(NTAP), dma(NTAP), dma(3), dma(3), dma(3), dma(NI), dma(NI), dma(NI),
            dma(NI, 2, 2), dma(NI, 2, 2), dma(NI), dma(NTAP), dma(NTAP), dma(NTAP, NU), dma(NTAP, NU), dma(nr), dma(nr), dma(nr), dma(nr), dma(NTAP, NU),
        ],
        compiler_params=pltpu.CompilerParams(collective_id=0, has_side_effects=True, vmem_limit_bytes=67043328),
        name="conv_block",
    )(x, dz, w, ws, gamma, beta, gamma_s)


def solution(mesh):
    act_spec = P("stage", ("dp", "tp"), None, None, None)
    kernel_spec = P("stage", None, None, "tp", None)
    short_spec = P("stage", "tp", None)
    vec_spec = P("stage", "tp")
    grad_spec = P("stage", "dp", None, None, "tp")

    def device_step(act_in, w_conv, w_short, gamma, beta, gamma_s, grad_z):
        z, dx, dw, ds = finish(*block(act_in[0], grad_z[0], w_conv.reshape(9, HC, C), w_short[0], gamma, beta, gamma_s))
        return z[None], dx[None], dw.reshape(1, 3, 3, HC, C), ds[None]

    return jax.shard_map(device_step, mesh=mesh, in_specs=(act_spec, kernel_spec, short_spec, vec_spec, vec_spec, vec_spec, grad_spec), out_specs=(grad_spec, act_spec, kernel_spec, short_spec), check_vma=False)
```

time: 764 us -> 193 us (0.25)
  the two profiles are of different devices: /device:TPU:0 before, /device:TPU:3 now
where the time goes in v2:
time: 193 us
  Pallas kernels  192 us (99%)
    pallas_call x1, Pallas kernels, block(): pl.pallas_call(body, out_shape=(jax.ShapeDtypeStruct((2 * NI, SIDE, SIDE,...  182 us
    pallas_call x1, Pallas kernels, finish(): pl.pallas_call(finish_body, out_shape=tuple((jax.ShapeDtypeStruct(a.shape...  10.3 us

profile of v2, /device:TPU:3, one launch (start us, length us, event | category | flops | bytes accessed | tf_op | source)
XLA Modules:
  0.0 193.1 jit_solution(13025952203997561757)
XLA Ops:
  0.6 182.0 %conv_block.1 = (bf16[12,28,28,256]{3,2,1,0:T(8,128)(2,1)}, bf16[6,28,28,512]{3,2,1,0:T(8,128)(2,1)}, f32[9,256,512]{2,1,0:T(8,128)}, f32[256,512]{1,0:T(8,128)}) custom-call(bf16[6,28,28,512]{3,2,1,0:T(8,128)(2,1)} %bitcast.8, bf16[12,28,28,256]{3,2,1,0:T(8,128)(2,1)} %bitcast.9, bf16[9,256,512]{2,1,0:T(8,128)(2,1)} %bitcast.10, bf16[256,512]{1,0:T(8,128)(2,1)} %bitcast.11, ...), custom_call_target="tpu_custom_call" | custom-call | tf_op jit(solution)/shard_map/conv_block/pallas_call | solution.py:449
  182.7 10.3 %finish.1 = (bf16[12,28,28,256]{3,2,1,0:T(8,128)(2,1)}, bf16[6,28,28,512]{3,2,1,0:T(8,128)(2,1)}, f32[9,256,512]{2,1,0:T(8,128)}, f32[256,512]{1,0:T(8,128)}) custom-call(bf16[12,28,28,256]{3,2,1,0:T(8,128)(2,1)} %get-tuple-element.12.z_in, bf16[6,28,28,512]{3,2,1,0:T(8,128)(2,1)} %get-tuple-element.13.dx_in, f32[9,256,512]{2,1,0:T(8,128)} %get-tuple-element.14.dw_in, ...), custom_call_target="tpu_custom_call" | custom-call | tf_op jit(solution)/shard_map/finish/pallas_call | solution.py:433

commit v3 on v2

--- a/solution.py
+++ b/solution.py
@@ -20,10 +20,10 @@
 DXCHUNKS = ((0, 384), (384, 512))
 NTAP = 10
 UNIT = 64
-NU = HC // UNIT
-RELAYED = tuple((m, s) for m in range(9) for s in range(2))[:18]
-STRAIGHT = tuple((m, s) for m in range(NTAP) for s in range(NU) if (m, s) not in RELAYED)
-ARRIVAL = sorted([(i + 1, u) for i, u in enumerate(STRAIGHT)] + [(i + 5.5, u) for i, u in enumerate(RELAYED)])
+RELAYED = tuple((m, s * UNIT, UNIT) for m in range(9) for s in range(2))
+STRAIGHT = tuple((m, 2 * UNIT, 2 * UNIT) for m in range(9)) + ((9, 0, 2 * UNIT), (9, 2 * UNIT, 2 * UNIT))
+UNITS = RELAYED + STRAIGHT
+ARRIVAL = sorted([(2 * i + 2, u) for i, u in enumerate(STRAIGHT)] + [(i + 5.5, u) for i, u in enumerate(RELAYED)])
 SPLIT = 5
 
 
@@ -81,24 +81,23 @@
         return rcopy(xr.at[k, at, h * HC:(h + 1) * HC], dzv.at[k, h, at], dxs.at[k, c, h], dxr.at[k, c, h], p_x)
 
     def unit_rows(u):
-        return pl.ds(pl.multiple_of(tp * HC + u[1] * UNIT, UNIT), UNIT)
+        return pl.ds(pl.multiple_of(tp * HC + u[1], UNIT), u[2])
 
     def part(ref, u):
-        return ref.at[u[0], u[1] * UNIT:(u[1] + 1) * UNIT]
+        return ref.at[u[0], u[1]:u[1] + u[2]]
 
     def held(ref, n):
-        return part(ref, divmod(n, NU))
+        return part(ref, (n // 4, n % 4 * UNIT, UNIT))
 
     def relay_a(n):
-        m, s = RELAYED[n]
-        return rcopy(acc.at[m, unit_rows((m, s))], held(tpr, n), ys.at[m, s], rar.at[n], p_x)
+        u = RELAYED[n]
+        return rcopy(acc.at[u[0], unit_rows(u)], held(tpr, n), ys.at[n], rar.at[n], p_x)
 
     def relay_b(n):
         return rcopy(held(tpr, n), held(dpr, n), ras.at[n], rbr.at[n], p_d)
 
     def relay_c(n):
-        m, s = RELAYED[n]
-        return rcopy(held(dpr, n), part(dpr, (m, s)), rbs.at[n], yr.at[m, s], p_x)
+        return rcopy(held(dpr, n), part(dpr, RELAYED[n]), rbs.at[n], yr.at[n], p_x)
 
     widen[...] = select((BLK, PBLK), 0)
     pack[...] = select((PBLK, BLK), 1)
@@ -110,7 +109,6 @@
         gs[...] = jnp.zeros((ROWS, C), BF16)
         load_part(0)
         pack_part(0, 0)
-        pack_part(0, 1)
 
     pl.semaphore_wait(barrier, 3)
 
@@ -120,6 +118,7 @@
             return pltpu.make_async_copy(xraw.at[k % 2], dx_out.at[k], dxo.at[k])
 
         x_copy(0, 0).start()
+        pack_part(0, 1)
         x_copy(0, 1).start()
         for k in range(1, NI):
             load_part(k)
@@ -209,13 +208,13 @@
             return rcopy(acc.at[m, other], tpr.at[m], ts.at[m], tr.at[m], p_t)
 
         def y_copy(u):
-            return rcopy(acc.at[u[0], unit_rows(u)], part(dpr, u), ys.at[u[0], u[1]], yr.at[u[0], u[1]], p_d)
+            n = UNITS.index(u)
+            return rcopy(acc.at[u[0], unit_rows(u)], part(dpr, u), ys.at[n], yr.at[n], p_d)
 
         def out_copy(u):
-            m, s = u
-            rows = slice(s * UNIT, (s + 1) * UNIT)
-            dst = ds_out.at[rows] if m == 9 else dw_out.at[m, rows]
-            return pltpu.make_async_copy(part(tpr, u), dst, ol.at[m, s])
+            rows = slice(u[1], u[1] + u[2])
+            dst = ds_out.at[rows] if u[0] == 9 else dw_out.at[u[0], rows]
+            return pltpu.make_async_copy(part(tpr, u), dst, ol.at[UNITS.index(u)])
 
         for k in range(2):
             for q in range(2):
@@ -278,14 +277,10 @@
 
         def pass_on(m):
             t_copy(m).wait_recv()
-            for s in range(NU):
-                u = (m, s)
-                rows = unit_rows(u)
-                acc[m, rows] = acc[m, rows] + tpr[m, s * UNIT:(s + 1) * UNIT]
-                if u in RELAYED:
-                    relay_a(RELAYED.index(u)).start()
-                else:
-                    y_copy(u).start()
+            for u in UNITS:
+                if u[0] == m:
+                    acc[m, unit_rows(u)] = acc[m, unit_rows(u)] + part(tpr, u)[...]
+                    relay_a(RELAYED.index(u)).start() if u in RELAYED else y_copy(u).start()
 
         def forward(k, blocks, r, n):
             for b in blocks:
@@ -346,10 +341,9 @@
                         acc[m] += dot(xt[...], gcat[at:at + ROWS, j * C:(j + 1) * C])
                     if last:
                         t_copy(m).start()
-                        if m >= 2:
-                            pass_on(m - 2)
+                        if m >= 1:
+                            pass_on(m - 1)
                 if last:
-                    pass_on(NTAP - 2)
                     pass_on(NTAP - 1)
 
             if last:
@@ -367,15 +361,14 @@
 
         for _, u in ARRIVAL:
             y_copy(u).wait_recv()
-            m, s = u
-            tpr[m, s * UNIT:(s + 1) * UNIT] = acc[m, unit_rows(u)] + part(dpr, u)[...]
+            tpr[u[0], u[1]:u[1] + u[2]] = acc[u[0], unit_rows(u)] + part(dpr, u)[...]
             out_copy(u).start()
 
         for m in range(NTAP):
             t_copy(m).wait_send()
-            for s in range(NU):
-                y_copy((m, s)).wait_send()
-                out_copy((m, s)).wait()
+        for u in UNITS:
+            y_copy(u).wait_send()
+            out_copy(u).wait()
 
         for k in range(NI - 2, NI):
             z_local(k).wait()
@@ -479,7 +472,7 @@
             pltpu.VMEM((BLK, PBLK), BF16),
             pltpu.VMEM((PBLK, BLK), BF16),
             dma(NI, 2), dma(NI, 2), dma(NI), dma(NI, 2), dma(NI), dma(NI), dma(NTAP), dma(NTAP), dma(NTAP), dma(3), dma(3), dma(3), dma(NI), dma(NI), dma(NI),
-            dma(NI, 2, 2), dma(NI, 2, 2), dma(NI), dma(NTAP), dma(NTAP), dma(NTAP, NU), dma(NTAP, NU), dma(nr), dma(nr), dma(nr), dma(nr), dma(NTAP, NU),
+            dma(NI, 2, 2), dma(NI, 2, 2), dma(NI), dma(NTAP), dma(NTAP), dma(len(UNITS)), dma(len(UNITS)), dma(nr), dma(nr), dma(nr), dma(nr), dma(len(UNITS)),
         ],
         compiler_params=pltpu.CompilerParams(collective_id=0, has_side_effects=True, vmem_limit_bytes=67043328),
         name="conv_block",

time: 193 us -> 192 us (level)
  no operation moved by 1% of the time
where the time goes in v3:
time: 192 us
  Pallas kernels  191 us (99%)
    pallas_call x1, Pallas kernels, block(): pl.pallas_call(body, out_shape=(jax.ShapeDtypeStruct((2 * NI, SIDE, SIDE,...  181 us
    pallas_call x1, Pallas kernels, finish(): pl.pallas_call(finish_body, out_shape=tuple((jax.ShapeDtypeStruct(a.shape...  10.3 us

profile of v3, /device:TPU:3, one launch (start us, length us, event | category | flops | bytes accessed | tf_op | source)
XLA Modules:
  0.0 192.3 jit_solution(1367684748218101796)
XLA Ops:
  0.6 181.2 %conv_block.1 = (bf16[12,28,28,256]{3,2,1,0:T(8,128)(2,1)}, bf16[6,28,28,512]{3,2,1,0:T(8,128)(2,1)}, f32[9,256,512]{2,1,0:T(8,128)}, f32[256,512]{1,0:T(8,128)}) custom-call(bf16[6,28,28,512]{3,2,1,0:T(8,128)(2,1)} %bitcast.8, bf16[12,28,28,256]{3,2,1,0:T(8,128)(2,1)} %bitcast.9, bf16[9,256,512]{2,1,0:T(8,128)(2,1)} %bitcast.10, bf16[256,512]{1,0:T(8,128)(2,1)} %bitcast.11, ...), custom_call_target="tpu_custom_call" | custom-call | tf_op jit(solution)/shard_map/conv_block/pallas_call | solution.py:442
  181.8 10.3 %finish.1 = (bf16[12,28,28,256]{3,2,1,0:T(8,128)(2,1)}, bf16[6,28,28,512]{3,2,1,0:T(8,128)(2,1)}, f32[9,256,512]{2,1,0:T(8,128)}, f32[256,512]{1,0:T(8,128)}) custom-call(bf16[12,28,28,256]{3,2,1,0:T(8,128)(2,1)} %get-tuple-element.12.z_in, bf16[6,28,28,512]{3,2,1,0:T(8,128)(2,1)} %get-tuple-element.13.dx_in, f32[9,256,512]{2,1,0:T(8,128)} %get-tuple-element.14.dw_in, ...), custom_call_target="tpu_custom_call" | custom-call | tf_op jit(solution)/shard_map/finish/pallas_call | solution.py:426
